TPU v7x, 32 devices: a whole 2x2x4 slice. The times are simulated.
32 devices in a mesh: gy: 8 (over z, x), gx: 4 (over y, core).
Axes of the slice: x: 2, y: 2, z: 4, core: 2. Of those that a mesh axis runs over, the one named last changes fastest.
Arguments:
- right_side: float32 [32, 512, 512], P(None, 'gy', 'gx'), may hold values from -32 to 32
- couplings: float32 [3, 512, 512], P(None, 'gy', 'gx'), may hold values from 0.1 to 0.5
- center: float32 [512, 512], P('gy', 'gx'), may hold values from 0.6 to 1.5
- ocean_mask: int32 [512, 512], P('gy', 'gx'), may hold values 0 or 1
Outputs:
- solution: float32 [32, 512, 512], P(None, 'gy', 'gx')
- residual: float32 [32, 512, 512], P(None, 'gy', 'gx')
All inputs are finite; a program needn't handle non-finite values. No bound on the sum of `ocean_mask` on one device may be relied on, other than what follows from the above.
Results may differ from a plain program's by a relative error of at most 0.0055.
Values sent between devices are 32-bit elements; how exact they have to be, the bound alone decides.
A program may use at most 64 MiB of HBM per device.

v0:
```python
import jax
import jax.numpy as jnp
from jax import lax
from jax.experimental import pallas as pl
from jax.experimental.pallas import tpu as pltpu
from jax.sharding import PartitionSpec as P

ITERS = 6
HALO = 8
SHIFT = 0.1
LAG = 0.05
OPPOSITE = (1, 0, 3, 2, 7, 6, 5, 4)
PAIRS = [(i, j) for i in range(ITERS) for j in range(i, ITERS + 1)]


def passed_along(value, axis, steps):
    count = lax.axis_size(axis)
    first, last = (max(0, -steps), min(count, count - steps))
    return lax.ppermute(value, axis, [(source, source + steps) for source in range(first, last)])


def around(value, axis, steps):
    count = lax.axis_size(axis)
    return lax.ppermute(value, axis, [(i, (i + steps) % count) for i in range(count)])


def coupling_terms(couplings):
    south_rows = passed_along(couplings[:, -1:, :], "gy", 1)
    extended = jnp.concatenate([south_rows, couplings], axis=1)
    west_column = around(extended[:, :, -1:], "gx", 1)
    widened = jnp.concatenate([west_column, extended], axis=2)
    return (
        widened[0, 1:, 1:],
        widened[0, :-1, 1:],
        widened[1, 1:, 1:],
        widened[1, 1:, :-1],
        widened[2, 1:, 1:],
        widened[2, :-1, 1:],
        widened[2, 1:, :-1],
        widened[2, :-1, :-1],
    )


def basis_kernel(members, rows, main_ref, side_ref, diag_ref, basis_ref, gram_ref, sides):
    tiles = rows // 8
    lanes = lax.broadcasted_iota(jnp.int32, (8, 128), 1)
    first, last = lanes == 0, lanes == 127

    def field(k, m):
        return main_ref.at[m] if k == 0 else basis_ref.at[k - 1, m]

    def side(k, m):
        return side_ref.at[m] if k == 0 else sides.at[k - 1, m]

    for k in range(ITERS):
        for tile in range(tiles):
            base = 8 * tile
            cm = [main_ref[members + d, base : base + 8, :] for d in range(8)]
            cs = [side_ref[members + d, base : base + 8, :] for d in range(8)]

            def east(a, b):
                return jnp.where(last, pltpu.roll(b, 127, 1), pltpu.roll(a, 127, 1))

            def west(a, b):
                return jnp.where(first, pltpu.roll(b, 1, 1), pltpu.roll(a, 1, 1))

            for d in (2, 4, 5):
                cm[d], cs[d] = west(cm[d], cs[d]), west(cs[d], cm[d])
            for d in (3, 6, 7):
                cm[d], cs[d] = east(cm[d], cs[d]), east(cs[d], cm[d])

            @pl.loop(0, members)
            def _(m):
                mids, easts, wests = [], [], []
                for get, c in ((field, cm), (side, cs)):
                    v = get(k, m)
                    mid = v[base : base + 8, :]
                    down = v[base - 1 : base + 7, :] if tile > 0 else pltpu.roll(mid, 1, 0)
                    up = v[base + 1 : base + 9, :] if tile < tiles - 1 else pltpu.roll(mid, 7, 0)
                    centre = c[0] * up + c[1] * down - SHIFT * mid
                    if k:
                        centre = centre - LAG * get(k - 1, m)[base : base + 8, :]
                    mids.append(centre)
                    easts.append(c[2] * mid + c[4] * up + c[5] * down)
                    wests.append(c[3] * mid + c[6] * up + c[7] * down)
                em, es = easts
                wm, ws = wests
                rem, res = pltpu.roll(em, 127, 1), pltpu.roll(es, 127, 1)
                rwm, rws = pltpu.roll(wm, 1, 1), pltpu.roll(ws, 1, 1)
                out = mids[0] + jnp.where(last, res, rem) + jnp.where(first, rws, rwm)
                basis_ref[k, m, base : base + 8, :] = out
                if k + 1 < ITERS:
                    out = mids[1] + jnp.where(last, rem, res) + jnp.where(first, rwm, rws)
                    sides[k, m, base : base + 8, :] = out

    @pl.loop(0, members)
    def _(m):
        sums = [None] * len(PAIRS)
        for tile in range(tiles - 2):
            base = HALO + 8 * tile
            diag = diag_ref[8 * tile : 8 * tile + 8, :]
            vs = [field(k, m)[base : base + 8, :] for k in range(ITERS + 1)]
            scaled = [diag * v for v in vs[:ITERS]]
            for n, (i, j) in enumerate(PAIRS):
                term = scaled[i] * vs[j]
                sums[n] = term if sums[n] is None else sums[n] + term
        for n in range(len(PAIRS)):
            gram_ref[n, pl.ds(m, 1), :] = jnp.sum(sums[n], axis=0, keepdims=True)


def coefficients(gram):
    def g(i, j):
        return gram[min(i, j)][max(i, j)]

    def applied(p):
        q = []
        for k in range(ITERS + 1):
            terms = []
            if k < len(p):
                terms.append((1.0 - SHIFT) * p[k])
            if 0 < k <= len(p):
                terms.append(-p[k - 1])
            if k + 1 < len(p):
                terms.append(-LAG * p[k + 1])
            if terms:
                q.append(sum(terms[1:], terms[0]))
        return q

    def inner(p, q):
        total = None
        for i, a in enumerate(p):
            row = None
            for j, b in enumerate(q):
                t = g(i, j) * b
                row = t if row is None else row + t
            t = a * row
            total = t if total is None else total + t
        return total

    one = jnp.ones_like(gram[0][0])
    z, p, x = [one], [one], []
    rz = g(0, 0)
    for iteration in range(ITERS):
        q = applied(p)
        step = rz / inner(p, q)
        x = [(x[k] if k < len(x) else 0.0) + step * p[k] for k in range(len(p))]
        z = [(z[k] if k < len(z) else 0.0) - step * q[k] for k in range(len(q))]
        if iteration + 1 < ITERS:
            rz_new = inner(z, z)
            beta = rz_new / rz
            p = [z[k] + (beta * p[k] if k < len(p) else 0.0) for k in range(len(z))]
            rz = rz_new
    return x, z


def combine_kernel(members, rows, z_ref, basis_ref, scale_ref, sum_ref, x_ref, r_ref, cx, cz):
    gram = [[None] * (ITERS + 1) for _ in range(ITERS + 1)]
    for n, (i, j) in enumerate(PAIRS):
        gram[i][j] = jnp.broadcast_to(sum_ref[:, n : n + 1], (members, 128))
    x, z = coefficients(gram)
    for k in range(ITERS):
        cx[k] = x[k]
    for k in range(ITERS + 1):
        cz[k] = z[k]

    @pl.loop(0, members)
    def _(m):
        xs = [jnp.broadcast_to(cx[k, pl.ds(m, 1), :], (8, 128)) for k in range(ITERS)]
        zs = [jnp.broadcast_to(cz[k, pl.ds(m, 1), :], (8, 128)) for k in range(ITERS + 1)]
        for base in range(0, rows, 8):
            at = slice(base + HALO, base + HALO + 8)
            vs = [z_ref[m, at, :]] + [basis_ref[k, m, at, :] for k in range(ITERS)]
            x_ref[m, base : base + 8, :] = sum((xs[k] * vs[k] for k in range(1, ITERS)), xs[0] * vs[0])
            total = sum((zs[k] * vs[k] for k in range(1, ITERS + 1)), zs[0] * vs[0])
            r_ref[m, base : base + 8, :] = scale_ref[base : base + 8, :] * total


def on_device(right_side, couplings, center, ocean_mask):
    members, rows, columns = right_side.shape
    oceanf = ocean_mask.astype(jnp.float32)
    terms = coupling_terms(couplings)
    diag = center + sum(terms[1:], terms[0])
    inverse = oceanf / diag
    planes = jnp.concatenate([right_side * inverse, jnp.stack(terms) * inverse], axis=0)
    edge = planes[:, -HALO:, :]
    south = passed_along(edge, "gy", 1)
    north = passed_along(planes[:, :HALO, :], "gy", -1)
    turned = jnp.concatenate([edge[:members]] + [edge[members + d][None] for d in OPPOSITE])
    turned = turned[:, ::-1, ::-1]
    count = lax.axis_size("gx")
    folded = lax.ppermute(turned, "gx", [(i, count - 1 - i) for i in range(count)])
    top = lax.axis_index("gy") == lax.axis_size("gy") - 1
    north = jnp.where(top, folded, north)
    main = jnp.concatenate([south, planes, north], axis=1)
    total = rows + 2 * HALO
    west = around(jnp.transpose(main[:, :, -HALO:], (2, 0, 1)), "gx", 1)
    east = around(jnp.transpose(main[:, :, :HALO], (2, 0, 1)), "gx", -1)
    gap = jnp.zeros((members + 8, total, columns - 2 * HALO), jnp.float32)
    side = jnp.concatenate(
        [jnp.transpose(east, (1, 2, 0)), gap, jnp.transpose(west, (1, 2, 0))], axis=2
    )
    vmem = pl.BlockSpec(memory_space=pltpu.VMEM)

    def first(*refs):
        basis_kernel(members, total, *refs)

    basis, gram = pl.pallas_call(
        first,
        out_shape=(
            jax.ShapeDtypeStruct((ITERS, members, total, columns), jnp.float32),
            jax.ShapeDtypeStruct((len(PAIRS), members, columns), jnp.float32),
        ),
        in_specs=[vmem] * 3,
        out_specs=(vmem, vmem),
        scratch_shapes=[pltpu.VMEM((ITERS - 1, members, total, columns), jnp.float32)],
    )(main, side, diag)
    sums = lax.psum(jnp.sum(gram, axis=2).T, ("gy", "gx"))

    def second(*refs):
        combine_kernel(members, rows, *refs)

    return pl.pallas_call(
        second,
        out_shape=(jax.ShapeDtypeStruct(right_side.shape, jnp.float32),) * 2,
        in_specs=[vmem] * 4,
        out_specs=(vmem, vmem),
        scratch_shapes=[
            pltpu.VMEM((ITERS, members, columns), jnp.float32),
            pltpu.VMEM((ITERS + 1, members, columns), jnp.float32),
        ],
    )(main, basis, oceanf * diag, sums)


def solution(mesh):
    in_specs = (P(None, "gy", "gx"), P(None, "gy", "gx"), P("gy", "gx"), P("gy", "gx"))
    out_specs = (P(None, "gy", "gx"), P(None, "gy", "gx"))
    return jax.shard_map(
        on_device, mesh=mesh, in_specs=in_specs, out_specs=out_specs, check_vma=False
    )
```

profile of v0, /device:TPU:0, one launch (start us, length us, event | category | flops | bytes accessed | tf_op | source)
XLA Modules:
  0.0 248.5 jit_solution(17313806041128499476)
XLA Ops:
  0.6 0.0 copy-start.1
  0.6 0.8 slice.88
  1.4 4.9 %collective-permute-start = (f32[3,1,128]{2,1,0:T(1,128)S(1)}, f32[3,1,128]{2,1,0:T(1,128)S(1)}, u32[]{:S(2)}, u32[]{:S(2)}) collective-permute-start(f32[3,1,128]{2,1,0:T(1,128)S(1)} %slice.88), channel_id=1, source_target_pairs={{0,4},{4,8},{8,12},{12,16},{16,20},{20,24},{24,28},{1,5},{5,9},{9,... | collective-permute-start | bytes 4616 | tf_op jit(solution)/shard_map/ppermute | solution.py:19
  6.3 1.3 collective-permute-done
  7.6 1.0 slice_maximum_fusion
  8.6 0.1 collective-permute-start.1
  8.6 0.8 constant_dynamic-update-slice_fusion.7
  9.4 3.4 %collective-permute-done.1 = f32[3,65,1]{2,1,0:T(8,128)S(1)} collective-permute-done((f32[3,65,1]{2,1,0:T(8,128)S(1)}, f32[3,65,1]{2,1,0:T(8,128)S(1)}, u32[]{:S(2)}, u32[]{:S(2)}) %collective-permute-start.1) | collective-permute-done | bytes 812 | tf_op jit(solution)/shard_map/ppermute | solution.py:24
  12.8 1.6 convert_multiply_fusion
  14.4 0.0 copy-start.2
  14.4 0.8 convert_divide_fusion
  15.2 0.8 constant_dynamic-update-slice_fusion.5
  16.0 0.8 constant_dynamic-update-slice_fusion.3
  16.8 0.0 copy-done.1
  16.8 0.1 broadcast_multiply_fusion
  16.9 0.0 copy-done.2
  17.1 0.1 rev.3
  17.2 0.1 collective-permute-start.3
  17.3 1.3 collective-permute-start.4
  18.6 4.8 %collective-permute-start.2 = (f32[40,8,128]{2,1,0:T(8,128)S(1)}, f32[40,8,128]{2,1,0:T(8,128)S(1)}, u32[]{:S(2)}, u32[]{:S(2)}) collective-permute-start(f32[40,8,128]{2,1,0:T(8,128)S(1)} %get-tuple-element.15), channel_id=1, source_target_pairs={{0,4},{4,8},{8,12},{12,16},{16,20},{20,24},{24,28},{1,5},{5,9},{9,... | collective-permute-start | bytes 491528 | tf_op jit(solution)/shard_map/ppermute | solution.py:19
  23.4 0.3 collective-permute-done.3
  23.7 1.9 collective-permute-done.4
  25.6 4.8 %collective-permute-done.2 = f32[40,8,128]{2,1,0:T(8,128)S(1)} collective-permute-done((f32[40,8,128]{2,1,0:T(8,128)S(1)}, f32[40,8,128]{2,1,0:T(8,128)S(1)}, u32[]{:S(2)}, u32[]{:S(2)}) %collective-permute-start.2) | collective-permute-done | bytes 163872 | tf_op jit(solution)/shard_map/ppermute | solution.py:19
  30.4 0.1 pad_maximum_fusion.refs_0_
  30.5 0.0 copy-start
  30.5 0.5 slice_bitcast_fusion.1
  31.0 0.7 copy-done
  31.8 0.5 copy.6
  32.2 0.9 collective-permute-start.5
  33.1 0.5 copy.8
  33.6 0.0 collective-permute-start.6
  33.6 0.1 pad.1.clone
  33.7 3.1 %collective-permute-done.5 = f32[8,40,80]{2,1,0:T(8,128)S(1)} collective-permute-done((f32[8,40,80]{2,1,0:T(8,128)S(1)}, f32[8,40,80]{2,1,0:T(8,128)S(1)}, u32[]{:S(2)}, u32[]{:S(2)}) %collective-permute-start.5) | collective-permute-done | bytes 102432 | tf_op jit(solution)/shard_map/ppermute | solution.py:24
  36.9 0.5 copy.7
  37.4 1.9 collective-permute-done.6
  39.3 1.4 copy.9
  40.7 1.6 pad_maximum_fusion.1.refs_1_
  42.3 157.4 %shard_map.59 = (f32[6,32,80,128]{3,2,1,0:T(8,128)}, f32[27,32,128]{2,1,0:T(8,128)}) custom-call(f32[40,80,128]{2,1,0:T(8,128)} %copy-done, f32[40,80,128]{2,1,0:T(8,128)} %pad_maximum_fusion.1.refs_1_, f32[64,128]{1,0:T(8,128)} %copy-done.2), custom_call_target="tpu_custom_call" | custom-call | tf_op jit(solution)/shard_map/pallas_call | solution.py:207
  199.7 1.2 reduce_sum.9
  200.9 0.1 copy.10
  201.0 40.9 %psum.7.refs_3_ = f32[32,27]{1,0:T(8,128)} all-reduce(f32[32,27]{1,0:T(8,128)S(1)} %bitcast.12), channel_id=1, replica_groups=mesh['gy'=8,'gx'=4] {'gy','gx'}, use_global_device_ids=true, to_apply=%region_1.2 | all-reduce | flops 864 | bytes 6912 | tf_op jit(solution)/shard_map/psum | solution.py:217
  241.9 6.6 %shard_map.60 = (f32[32,64,128]{2,1,0:T(8,128)}, f32[32,64,128]{2,1,0:T(8,128)}) custom-call(f32[40,80,128]{2,1,0:T(8,128)} %copy-done, f32[6,32,80,128]{3,2,1,0:T(8,128)} %get-tuple-element.4.refs_1_, f32[64,128]{1,0:T(8,128)} %get-tuple-element.6.refs_2_, f32[32,27]{1,0:T(8,128)} %psum.7.refs_3_), custom_call_target="tpu_custom_call" | custom-call | tf_op jit(solution)/shard_map/pallas_call | solution.py:222
  (18 shorter events, 0.1 us)
Async XLA Ops:
  0.6 16.2 %copy-start.1 = (f32[32,64,128]{2,1,0:T(8,128)S(1)}, f32[32,64,128]{2,1,0:T(8,128)}, u32[]{:S(2)}) copy-start(f32[32,64,128]{2,1,0:T(8,128)} %param.4) | copy-start | bytes 3145732
  1.4 6.2 %collective-permute-start = (f32[3,1,128]{2,1,0:T(1,128)S(1)}, f32[3,1,128]{2,1,0:T(1,128)S(1)}, u32[]{:S(2)}, u32[]{:S(2)}) collective-permute-start(f32[3,1,128]{2,1,0:T(1,128)S(1)} %slice.88), channel_id=1, source_target_pairs={{0,4},{4,8},{8,12},{12,16},{16,20},{20,24},{24,28},{1,5},{5,9},{9,... | collective-permute-start | bytes 4616 | tf_op jit(solution)/shard_map/ppermute | solution.py:19
  8.6 4.2 %collective-permute-start.1 = (f32[3,65,1]{2,1,0:T(8,128)S(1)}, f32[3,65,1]{2,1,0:T(8,128)S(1)}, u32[]{:S(2)}, u32[]{:S(2)}) collective-permute-start(f32[3,65,1]{2,1,0:T(8,128)S(1)} %slice_maximum_fusion), channel_id=1, source_target_pairs={{0,1},{1,2},{2,3},{3,0},{4,5},{5,6},{6,7},{7,4},{8,9},{9,10},{10,1... | collective-permute-start | bytes 2348 | tf_op jit(solution)/shard_map/ppermute | solution.py:24
  14.4 2.5 %copy-start.2 = (f32[64,128]{1,0:T(8,128)}, f32[64,128]{1,0:T(8,128)S(1)}, u32[]{:S(2)}) copy-start(f32[64,128]{1,0:T(8,128)S(1)} %get-tuple-element.7.refs_2_) | copy-start | bytes 98308
  17.2 6.5 %collective-permute-start.3 = (f32[40,8,128]{2,1,0:T(8,128)S(1)}, f32[40,8,128]{2,1,0:T(8,128)S(1)}, u32[]{:S(2)}, u32[]{:S(2)}) collective-permute-start(f32[40,8,128]{2,1,0:T(8,128)S(1)} %rev.3), channel_id=1, source_target_pairs={{0,3},{1,2},{2,1},{3,0},{4,7},{5,6},{6,5},{7,4},{8,11},{9,10},{10,... | collective-permute-start | bytes 491528 | tf_op jit(solution)/shard_map/ppermute | solution.py:191
  17.3 8.3 %collective-permute-start.4 = (f32[40,8,128]{2,1,0:T(8,128)S(1)}, f32[40,8,128]{2,1,0:T(8,128)S(1)}, u32[]{:S(2)}, u32[]{:S(2)}) collective-permute-start(f32[40,8,128]{2,1,0:T(8,128)S(1)} %get-tuple-element.16), channel_id=1, source_target_pairs={{4,0},{8,4},{12,8},{16,12},{20,16},{24,20},{28,24},{5,1},{9,5},{13... | collective-permute-start | bytes 491528 | tf_op jit(solution)/shard_map/ppermute | solution.py:19
  18.6 11.8 %collective-permute-start.2 = (f32[40,8,128]{2,1,0:T(8,128)S(1)}, f32[40,8,128]{2,1,0:T(8,128)S(1)}, u32[]{:S(2)}, u32[]{:S(2)}) collective-permute-start(f32[40,8,128]{2,1,0:T(8,128)S(1)} %get-tuple-element.15), channel_id=1, source_target_pairs={{0,4},{4,8},{8,12},{12,16},{16,20},{20,24},{24,28},{1,5},{5,9},{9,... | collective-permute-start | bytes 491528 | tf_op jit(solution)/shard_map/ppermute | solution.py:19
  30.5 1.3 copy-start
  32.2 4.6 %collective-permute-start.5 = (f32[8,40,80]{2,1,0:T(8,128)S(1)}, f32[8,40,80]{2,1,0:T(8,128)S(1)}, u32[]{:S(2)}, u32[]{:S(2)}) collective-permute-start(f32[8,40,80]{2,1,0:T(8,128)S(1)} %copy.6), channel_id=1, source_target_pairs={{0,3},{1,0},{2,1},{3,2},{4,7},{5,4},{6,5},{7,6},{8,11},{9,8},{10,9... | collective-permute-start | bytes 307208 | tf_op jit(solution)/shard_map/ppermute | solution.py:24
  33.6 5.7 %collective-permute-start.6 = (f32[8,40,80]{2,1,0:T(8,128)S(1)}, f32[8,40,80]{2,1,0:T(8,128)}, u32[]{:S(2)}, u32[]{:S(2)}) collective-permute-start(f32[8,40,80]{2,1,0:T(8,128)S(1)} %copy.8), channel_id=1, source_target_pairs={{0,1},{1,2},{2,3},{3,0},{4,5},{5,6},{6,7},{7,4},{8,9},{9,10},{10,1... | collective-permute-start | bytes 307208 | tf_op jit(solution)/shard_map/ppermute | solution.py:24
where the time goes:
time: 249 us
  Pallas kernels  164 us (66%)
  blocking collectives  40.9 us (16%)
  waiting for transfers between devices  16.7 us (7%)
  starting transfers between devices  12 us (5%)
  local copies, waits for them, and re-layouts  7.5 us (3%)
  other arithmetic  6.49 us (3%)
    pallas_call x1, Pallas kernels, on_device(): pl.pallas_call(first, out_shape=(jax.ShapeDtypeStruct((ITERS, members, to...  157 us
    psum x1, blocking collectives, on_device(): sums = lax.psum(jnp.sum(gram, axis=2).T, ('gy', 'gx'))  40.9 us
    ppermute x3, starting transfers between devices, passed_along(): lax.ppermute(value, axis, [(source, source + steps) for source in range(f...  11 us
    ppermute x3, waiting for transfers between devices, around(): lax.ppermute(value, axis, [(i, (i + steps) % count) for i in range(count)])  8.43 us
    ppermute x3, waiting for transfers between devices, passed_along(): lax.ppermute(value, axis, [(source, source + steps) for source in range(f...  7.97 us
    pallas_call x1, Pallas kernels, on_device(): pl.pallas_call(second, out_shape=(jax.ShapeDtypeStruct(right_side.shape,...  6.63 us
  transfers between devices with their start and end apart: 7, of which 7 were waited for; matrix products, arithmetic and copies ran while one was open for 1% of the time, Pallas kernels for 0%

commit v1 on v0

--- a/solution.py
+++ b/solution.py
@@ -9,6 +9,7 @@
 HALO = 8
 SHIFT = 0.1
 LAG = 0.05
+TOGETHER = 4
 OPPOSITE = (1, 0, 3, 2, 7, 6, 5, 4)
 PAIRS = [(i, j) for i in range(ITERS) for j in range(i, ITERS + 1)]
 
@@ -41,7 +42,7 @@
     )
 
 
-def basis_kernel(members, rows, main_ref, side_ref, diag_ref, basis_ref, gram_ref, sides):
+def basis_kernel(members, rows, main_ref, side_ref, diag_ref, basis_ref, gram_ref, sides, gram):
     tiles = rows // 8
     lanes = lax.broadcasted_iota(jnp.int32, (8, 128), 1)
     first, last = lanes == 0, lanes == 127
@@ -69,29 +70,32 @@
             for d in (3, 6, 7):
                 cm[d], cs[d] = east(cm[d], cs[d]), east(cs[d], cm[d])
 
-            @pl.loop(0, members)
-            def _(m):
-                mids, easts, wests = [], [], []
-                for get, c in ((field, cm), (side, cs)):
-                    v = get(k, m)
-                    mid = v[base : base + 8, :]
-                    down = v[base - 1 : base + 7, :] if tile > 0 else pltpu.roll(mid, 1, 0)
-                    up = v[base + 1 : base + 9, :] if tile < tiles - 1 else pltpu.roll(mid, 7, 0)
-                    centre = c[0] * up + c[1] * down - SHIFT * mid
-                    if k:
-                        centre = centre - LAG * get(k - 1, m)[base : base + 8, :]
-                    mids.append(centre)
-                    easts.append(c[2] * mid + c[4] * up + c[5] * down)
-                    wests.append(c[3] * mid + c[6] * up + c[7] * down)
-                em, es = easts
-                wm, ws = wests
-                rem, res = pltpu.roll(em, 127, 1), pltpu.roll(es, 127, 1)
-                rwm, rws = pltpu.roll(wm, 1, 1), pltpu.roll(ws, 1, 1)
-                out = mids[0] + jnp.where(last, res, rem) + jnp.where(first, rws, rwm)
-                basis_ref[k, m, base : base + 8, :] = out
-                if k + 1 < ITERS:
-                    out = mids[1] + jnp.where(last, rem, res) + jnp.where(first, rwm, rws)
-                    sides[k, m, base : base + 8, :] = out
+            @pl.loop(0, members // TOGETHER)
+            def _(block):
+                outs = []
+                for within in range(TOGETHER):
+                    m = block * TOGETHER + within
+                    mids, easts, wests = [], [], []
+                    for get, c in ((field, cm), (side, cs)):
+                        v = get(k, m)
+                        mid = v[base : base + 8, :]
+                        down = v[base - 1 : base + 7, :] if tile > 0 else pltpu.roll(mid, 1, 0)
+                        up = v[base + 1 : base + 9, :] if tile < tiles - 1 else pltpu.roll(mid, 7, 0)
+                        centre = c[0] * up + c[1] * down - SHIFT * mid
+                        if k:
+                            centre = centre - LAG * get(k - 1, m)[base : base + 8, :]
+                        mids.append(centre)
+                        easts.append(c[2] * mid + c[4] * up + c[5] * down)
+                        wests.append(c[3] * mid + c[6] * up + c[7] * down)
+                    rem, res = [pltpu.roll(e, 127, 1) for e in easts]
+                    rwm, rws = [pltpu.roll(w, 1, 1) for w in wests]
+                    out_main = mids[0] + jnp.where(last, res, rem) + jnp.where(first, rws, rwm)
+                    out_side = mids[1] + jnp.where(last, rem, res) + jnp.where(first, rwm, rws)
+                    outs.append((m, out_main, out_side))
+                for m, out_main, out_side in outs:
+                    basis_ref[k, m, base : base + 8, :] = out_main
+                    if k + 1 < ITERS:
+                        sides[k, m, base : base + 8, :] = out_side
 
     @pl.loop(0, members)
     def _(m):
@@ -105,7 +109,69 @@
                 term = scaled[i] * vs[j]
                 sums[n] = term if sums[n] is None else sums[n] + term
         for n in range(len(PAIRS)):
-            gram_ref[n, pl.ds(m, 1), :] = jnp.sum(sums[n], axis=0, keepdims=True)
+            gram[n, pl.ds(m, 1), :] = jnp.sum(sums[n], axis=0, keepdims=True)
+
+    wide = lax.broadcasted_iota(jnp.int32, (members, 128), 1)
+    packed = jnp.zeros((members, 128), jnp.float32)
+    for n in range(len(PAIRS)):
+        packed = jnp.where(wide == n, jnp.sum(gram[n], axis=1, keepdims=True), packed)
+    gram_ref[...] = packed_in(packed)
+
+
+def packed_in(values):
+    members = values.shape[0]
+    groups = members // 8
+    width = 128 // groups
+    total = values[0:8]
+    for g in range(1, groups):
+        total = total + pltpu.roll(values[8 * g : 8 * g + 8], width * g, 1)
+    return total
+
+
+def unpacked(values, members):
+    groups = members // 8
+    width = 128 // groups
+    parts = [values] + [pltpu.roll(values, 128 - width * g, 1) for g in range(1, groups)]
+    return jnp.concatenate(parts, axis=0)
+
+
+def total_kernel(axes, counts, in_ref, out_ref, *scratch):
+    buffers, held = scratch[: len(axes)], scratch[len(axes)]
+    send_sems, recv_sems = scratch[len(axes) + 1 : 2 * len(axes) + 1], scratch[2 * len(axes) + 1 :]
+    barrier = pltpu.get_barrier_semaphore()
+    for axis, count in zip(axes, counts):
+        me = lax.axis_index(axis)
+        for step in range(1, count):
+            peer = lax.rem(me + step, count)
+            pl.semaphore_signal(
+                barrier, inc=1, device_id={axis: peer}, device_id_type=pl.DeviceIdType.MESH
+            )
+    pl.semaphore_wait(barrier, sum(counts) - len(counts))
+    for stage, (axis, count) in enumerate(zip(axes, counts)):
+        me = lax.axis_index(axis)
+        source = in_ref if stage == 0 else held
+        copies = []
+        for step in range(1, count):
+            peer = lax.rem(me + step, count)
+            copy = pltpu.make_async_remote_copy(
+                src_ref=source,
+                dst_ref=buffers[stage].at[step],
+                send_sem=send_sems[stage].at[step],
+                recv_sem=recv_sems[stage].at[step],
+                device_id={axis: peer},
+                device_id_type=pl.DeviceIdType.MESH,
+            )
+            copy.start()
+            copies.append(copy)
+        for copy in copies:
+            copy.wait()
+        total = source[...]
+        for step in range(1, count):
+            total = total + buffers[stage][step]
+        if stage + 1 < len(axes):
+            held[...] = total
+        else:
+            out_ref[...] = total
 
 
 def coefficients(gram):
@@ -155,8 +221,9 @@
 
 def combine_kernel(members, rows, z_ref, basis_ref, scale_ref, sum_ref, x_ref, r_ref, cx, cz):
     gram = [[None] * (ITERS + 1) for _ in range(ITERS + 1)]
+    sums = unpacked(sum_ref[...], members)
     for n, (i, j) in enumerate(PAIRS):
-        gram[i][j] = jnp.broadcast_to(sum_ref[:, n : n + 1], (members, 128))
+        gram[i][j] = jnp.broadcast_to(sums[:, n : n + 1], (members, 128))
     x, z = coefficients(gram)
     for k in range(ITERS):
         cx[k] = x[k]
@@ -173,6 +240,26 @@
             x_ref[m, base : base + 8, :] = sum((xs[k] * vs[k] for k in range(1, ITERS)), xs[0] * vs[0])
             total = sum((zs[k] * vs[k] for k in range(1, ITERS + 1)), zs[0] * vs[0])
             r_ref[m, base : base + 8, :] = scale_ref[base : base + 8, :] * total
+
+
+def totals(values):
+    axes = ("gx", "gy")
+    counts = [lax.axis_size(axis) for axis in axes]
+
+    def kernel(*refs):
+        total_kernel(axes, counts, *refs)
+
+    vmem = pl.BlockSpec(memory_space=pltpu.VMEM)
+    return pl.pallas_call(
+        kernel,
+        out_shape=jax.ShapeDtypeStruct(values.shape, jnp.float32),
+        in_specs=[vmem],
+        out_specs=vmem,
+        scratch_shapes=[pltpu.VMEM((count,) + values.shape, jnp.float32) for count in counts]
+        + [pltpu.VMEM(values.shape, jnp.float32)]
+        + [pltpu.SemaphoreType.DMA((count,)) for count in counts] * 2,
+        compiler_params=pltpu.CompilerParams(collective_id=0, has_side_effects=True),
+    )(values)
 
 
 def on_device(right_side, couplings, center, ocean_mask):
@@ -208,13 +295,16 @@
         first,
         out_shape=(
             jax.ShapeDtypeStruct((ITERS, members, total, columns), jnp.float32),
-            jax.ShapeDtypeStruct((len(PAIRS), members, columns), jnp.float32),
+            jax.ShapeDtypeStruct((8, 128), jnp.float32),
         ),
         in_specs=[vmem] * 3,
         out_specs=(vmem, vmem),
-        scratch_shapes=[pltpu.VMEM((ITERS - 1, members, total, columns), jnp.float32)],
+        scratch_shapes=[
+            pltpu.VMEM((ITERS - 1, members, total, columns), jnp.float32),
+            pltpu.VMEM((len(PAIRS), members, columns), jnp.float32),
+        ],
     )(main, side, diag)
-    sums = lax.psum(jnp.sum(gram, axis=2).T, ("gy", "gx"))
+    sums = totals(gram)
 
     def second(*refs):
         combine_kernel(members, rows, *refs)

time: 249 us -> 117 us (0.47)
  Pallas kernels: 164 us -> 73.6 us
  blocking collectives: 40.9 us -> 0 us
    pallas_call x1, Pallas kernels: 157 us -> 55.1 us  [on_device(): pl.pallas_call(first, out_shape=(jax.ShapeDtypeStruct((ITERS, members, to...]
    psum x1 -> x0, blocking collectives: 40.9 us -> none  [on_device(): sums = lax.psum(jnp.sum(gram, axis=2).T, ('gy', 'gx'))]
    pallas_call x0 -> x1, Pallas kernels: none -> 11.7 us  [totals(): pl.pallas_call(kernel, out_shape=jax.ShapeDtypeStruct(values.shape, jnp.f...]
  transfers between devices with their start and end apart: 7 -> 7, of which waited for: 7 -> 7; matrix products, arithmetic and copies ran while one was open for 1% -> 2% of each run, Pallas kernels for 0% -> 0%
where the time goes in v1:
time: 117 us; the launch traced here: 116 us
  Pallas kernels  73.6 us (63%)
  waiting for transfers between devices  16.7 us (14%)
  starting transfers between devices  12 us (10%)
  local copies, waits for them, and re-layouts  7.41 us (6%)
  other arithmetic  5.3 us (5%)
    pallas_call x1, Pallas kernels, on_device(): pl.pallas_call(first, out_shape=(jax.ShapeDtypeStruct((ITERS, members, to...  55.1 us
    pallas_call x1, Pallas kernels, totals(): pl.pallas_call(kernel, out_shape=jax.ShapeDtypeStruct(values.shape, jnp.f...  11.7 us
    ppermute x3, starting transfers between devices, passed_along(): lax.ppermute(value, axis, [(source, source + steps) for source in range(f...  11 us
    ppermute x3, waiting for transfers between devices, around(): lax.ppermute(value, axis, [(i, (i + steps) % count) for i in range(count)])  8.43 us
    ppermute x3, waiting for transfers between devices, passed_along(): lax.ppermute(value, axis, [(source, source + steps) for source in range(f...  7.97 us
    pallas_call x1, Pallas kernels, on_device(): pl.pallas_call(second, out_shape=(jax.ShapeDtypeStruct(right_side.shape,...  6.72 us
    unnamed x21, local copies, waits for them, and re-layouts  3.07 us
  transfers between devices with their start and end apart: 7, of which 7 were waited for; matrix products, arithmetic and copies ran while one was open for 2% of the time, Pallas kernels for 0%

profile of v1, /device:TPU:0, one launch (start us, length us, event | category | flops | bytes accessed | tf_op | source)
XLA Modules:
  0.0 115.9 jit_solution(16407166946771559134)
XLA Ops:
  0.6 0.0 copy-start.1
  0.6 0.8 slice.88
  1.4 4.9 %collective-permute-start = (f32[3,1,128]{2,1,0:T(1,128)S(1)}, f32[3,1,128]{2,1,0:T(1,128)S(1)}, u32[]{:S(2)}, u32[]{:S(2)}) collective-permute-start(f32[3,1,128]{2,1,0:T(1,128)S(1)} %slice.88), channel_id=1, source_target_pairs={{0,4},{4,8},{8,12},{12,16},{16,20},{20,24},{24,28},{1,5},{5,9},{9,... | collective-permute-start | bytes 4616 | tf_op jit(solution)/shard_map/ppermute | solution.py:20
  6.3 1.3 %collective-permute-done = f32[3,1,128]{2,1,0:T(1,128)S(1)} collective-permute-done((f32[3,1,128]{2,1,0:T(1,128)S(1)}, f32[3,1,128]{2,1,0:T(1,128)S(1)}, u32[]{:S(2)}, u32[]{:S(2)}) %collective-permute-start) | collective-permute-done | bytes 1568 | tf_op jit(solution)/shard_map/ppermute | solution.py:20
  7.6 1.0 slice_maximum_fusion
  8.6 0.1 collective-permute-start.1
  8.6 0.8 constant_dynamic-update-slice_fusion.7
  9.4 3.4 %collective-permute-done.1 = f32[3,65,1]{2,1,0:T(8,128)S(1)} collective-permute-done((f32[3,65,1]{2,1,0:T(8,128)S(1)}, f32[3,65,1]{2,1,0:T(8,128)S(1)}, u32[]{:S(2)}, u32[]{:S(2)}) %collective-permute-start.1) | collective-permute-done | bytes 812 | tf_op jit(solution)/shard_map/ppermute | solution.py:25
  12.8 1.6 %convert_multiply_fusion = (f32[64,128]{1,0:T(8,128)}, f32[64,128]{1,0:T(8,128)S(1)}, f32[1,64,128]{2,1,0:T(8,128)S(1)}, f32[1,64,128]{2,1,0:T(8,128)S(1)}, f32[...) fusion(s32[64,128]{1,0:T(8,128)} %param.7, f32[64,128]{1,0:T(8,128)} %param.6, ...), kind=kLoop, calls=%fused_computation.34 | loop fusion | flops 147456 | bytes 493836 | tf_op jit(solution)/shard_map/mul | solution.py:321
  14.4 0.0 copy-start.2
  14.4 0.8 convert_divide_fusion
  15.2 0.8 constant_dynamic-update-slice_fusion.5
  16.0 0.8 constant_dynamic-update-slice_fusion.3
  16.8 0.0 copy-done.1
  16.8 0.1 broadcast_multiply_fusion
  16.9 0.0 copy-done.2
  17.1 0.1 rev.3
  17.2 0.1 collective-permute-start.3
  17.3 1.3 %collective-permute-start.4 = (f32[40,8,128]{2,1,0:T(8,128)S(1)}, f32[40,8,128]{2,1,0:T(8,128)S(1)}, u32[]{:S(2)}, u32[]{:S(2)}) collective-permute-start(f32[40,8,128]{2,1,0:T(8,128)S(1)} %get-tuple-element.16), channel_id=1, source_target_pairs={{4,0},{8,4},{12,8},{16,12},{20,16},{24,20},{28,24},{5,1},{9,5},{13... | collective-permute-start | bytes 491528 | tf_op jit(solution)/shard_map/ppermute | solution.py:20
  18.6 4.8 %collective-permute-start.2 = (f32[40,8,128]{2,1,0:T(8,128)S(1)}, f32[40,8,128]{2,1,0:T(8,128)S(1)}, u32[]{:S(2)}, u32[]{:S(2)}) collective-permute-start(f32[40,8,128]{2,1,0:T(8,128)S(1)} %get-tuple-element.15), channel_id=1, source_target_pairs={{0,4},{4,8},{8,12},{12,16},{16,20},{20,24},{24,28},{1,5},{5,9},{9,... | collective-permute-start | bytes 491528 | tf_op jit(solution)/shard_map/ppermute | solution.py:20
  23.4 0.3 collective-permute-done.3
  23.7 1.9 %collective-permute-done.4 = f32[40,8,128]{2,1,0:T(8,128)S(1)} collective-permute-done((f32[40,8,128]{2,1,0:T(8,128)S(1)}, f32[40,8,128]{2,1,0:T(8,128)S(1)}, u32[]{:S(2)}, u32[]{:S(2)}) %collective-permute-start.4) | collective-permute-done | bytes 163872 | tf_op jit(solution)/shard_map/ppermute | solution.py:20
  25.6 4.8 %collective-permute-done.2 = f32[40,8,128]{2,1,0:T(8,128)S(1)} collective-permute-done((f32[40,8,128]{2,1,0:T(8,128)S(1)}, f32[40,8,128]{2,1,0:T(8,128)S(1)}, u32[]{:S(2)}, u32[]{:S(2)}) %collective-permute-start.2) | collective-permute-done | bytes 163872 | tf_op jit(solution)/shard_map/ppermute | solution.py:20
  30.4 0.1 pad_maximum_fusion.refs_0_
  30.5 0.0 copy-start
  30.5 0.5 slice_bitcast_fusion.1
  31.0 0.7 copy-done
  31.8 0.5 copy.6
  32.2 0.9 collective-permute-start.5
  33.1 0.5 copy.8
  33.6 0.0 collective-permute-start.6
  33.6 0.1 pad.1.clone
  33.7 3.1 %collective-permute-done.5 = f32[8,40,80]{2,1,0:T(8,128)S(1)} collective-permute-done((f32[8,40,80]{2,1,0:T(8,128)S(1)}, f32[8,40,80]{2,1,0:T(8,128)S(1)}, u32[]{:S(2)}, u32[]{:S(2)}) %collective-permute-start.5) | collective-permute-done | bytes 102432 | tf_op jit(solution)/shard_map/ppermute | solution.py:25
  36.8 0.5 copy.7
  37.4 1.9 %collective-permute-done.6 = f32[8,40,80]{2,1,0:T(8,128)} collective-permute-done((f32[8,40,80]{2,1,0:T(8,128)S(1)}, f32[8,40,80]{2,1,0:T(8,128)}, u32[]{:S(2)}, u32[]{:S(2)}) %collective-permute-start.6) | collective-permute-done | bytes 102432 | tf_op jit(solution)/shard_map/ppermute | solution.py:25
  39.3 1.4 %copy.9 = f32[8,40,80]{0,2,1:T(8,128)S(1)} copy(f32[8,40,80]{2,1,0:T(8,128)} %collective-permute-done.6) | data formatting | bytes 204800 | tf_op jit(solution)/shard_map/ppermute | solution.py:25
  40.7 1.7 %pad_maximum_fusion.1.refs_1_ = f32[40,80,128]{2,1,0:T(8,128)} fusion(f32[40,80,8]{2,1,0:T(8,128)S(1)} %bitcast.10, f32[40,80,8]{2,1,0:T(8,128)S(1)} %bitcast.9, f32[128]{0:T(128)S(1)} %pad.1.clone), kind=kLoop, calls=%fused_computation.3 | loop fusion | flops 819200 | bytes 1843712 | tf_op jit(solution)/shard_map/concatenate | solution.py:286
  42.3 55.1 %shard_map.59 = (f32[6,32,80,128]{3,2,1,0:T(8,128)}, f32[8,128]{1,0:T(8,128)}) custom-call(f32[40,80,128]{2,1,0:T(8,128)} %copy-done, f32[40,80,128]{2,1,0:T(8,128)} %pad_maximum_fusion.1.refs_1_, f32[64,128]{1,0:T(8,128)} %copy-done.2), custom_call_target="tpu_custom_call" | custom-call | tf_op jit(solution)/shard_map/pallas_call | solution.py:294
  97.5 11.7 %shard_map.60.refs_3_ = f32[8,128]{1,0:T(8,128)} custom-call(f32[8,128]{1,0:T(8,128)} %get-tuple-element.5.refs_0_), custom_call_target="tpu_custom_call" | custom-call | tf_op jit(solution)/shard_map/pallas_call | solution.py:253
  109.2 6.7 %shard_map.61 = (f32[32,64,128]{2,1,0:T(8,128)}, f32[32,64,128]{2,1,0:T(8,128)}) custom-call(f32[40,80,128]{2,1,0:T(8,128)} %copy-done, f32[6,32,80,128]{3,2,1,0:T(8,128)} %get-tuple-element.4.refs_1_, f32[64,128]{1,0:T(8,128)} %get-tuple-element.6.refs_2_, f32[8,128]{1,0:T(8,128)} %shard_map.60.refs_3_), custom_call_target="tpu_custom_call" | custom-call | tf_op jit(solution)/shard_map/pallas_call | solution.py:312
  (18 shorter events, 0.1 us)
Async XLA Ops:
  0.6 16.2 %copy-start.1 = (f32[32,64,128]{2,1,0:T(8,128)S(1)}, f32[32,64,128]{2,1,0:T(8,128)}, u32[]{:S(2)}) copy-start(f32[32,64,128]{2,1,0:T(8,128)} %param.4) | copy-start | bytes 3145732
  1.4 6.2 %collective-permute-start = (f32[3,1,128]{2,1,0:T(1,128)S(1)}, f32[3,1,128]{2,1,0:T(1,128)S(1)}, u32[]{:S(2)}, u32[]{:S(2)}) collective-permute-start(f32[3,1,128]{2,1,0:T(1,128)S(1)} %slice.88), channel_id=1, source_target_pairs={{0,4},{4,8},{8,12},{12,16},{16,20},{20,24},{24,28},{1,5},{5,9},{9,... | collective-permute-start | bytes 4616 | tf_op jit(solution)/shard_map/ppermute | solution.py:20
  8.6 4.2 %collective-permute-start.1 = (f32[3,65,1]{2,1,0:T(8,128)S(1)}, f32[3,65,1]{2,1,0:T(8,128)S(1)}, u32[]{:S(2)}, u32[]{:S(2)}) collective-permute-start(f32[3,65,1]{2,1,0:T(8,128)S(1)} %slice_maximum_fusion), channel_id=1, source_target_pairs={{0,1},{1,2},{2,3},{3,0},{4,5},{5,6},{6,7},{7,4},{8,9},{9,10},{10,1... | collective-permute-start | bytes 2348 | tf_op jit(solution)/shard_map/ppermute | solution.py:25
  14.4 2.5 %copy-start.2 = (f32[64,128]{1,0:T(8,128)}, f32[64,128]{1,0:T(8,128)S(1)}, u32[]{:S(2)}) copy-start(f32[64,128]{1,0:T(8,128)S(1)} %get-tuple-element.7.refs_2_) | copy-start | bytes 98308
  17.2 6.5 %collective-permute-start.3 = (f32[40,8,128]{2,1,0:T(8,128)S(1)}, f32[40,8,128]{2,1,0:T(8,128)S(1)}, u32[]{:S(2)}, u32[]{:S(2)}) collective-permute-start(f32[40,8,128]{2,1,0:T(8,128)S(1)} %rev.3), channel_id=1, source_target_pairs={{0,3},{1,2},{2,1},{3,0},{4,7},{5,6},{6,5},{7,4},{8,11},{9,10},{10,... | collective-permute-start | bytes 491528 | tf_op jit(solution)/shard_map/ppermute | solution.py:278
  17.3 8.3 %collective-permute-start.4 = (f32[40,8,128]{2,1,0:T(8,128)S(1)}, f32[40,8,128]{2,1,0:T(8,128)S(1)}, u32[]{:S(2)}, u32[]{:S(2)}) collective-permute-start(f32[40,8,128]{2,1,0:T(8,128)S(1)} %get-tuple-element.16), channel_id=1, source_target_pairs={{4,0},{8,4},{12,8},{16,12},{20,16},{24,20},{28,24},{5,1},{9,5},{13... | collective-permute-start | bytes 491528 | tf_op jit(solution)/shard_map/ppermute | solution.py:20
  18.6 11.8 %collective-permute-start.2 = (f32[40,8,128]{2,1,0:T(8,128)S(1)}, f32[40,8,128]{2,1,0:T(8,128)S(1)}, u32[]{:S(2)}, u32[]{:S(2)}) collective-permute-start(f32[40,8,128]{2,1,0:T(8,128)S(1)} %get-tuple-element.15), channel_id=1, source_target_pairs={{0,4},{4,8},{8,12},{12,16},{16,20},{20,24},{24,28},{1,5},{5,9},{9,... | collective-permute-start | bytes 491528 | tf_op jit(solution)/shard_map/ppermute | solution.py:20
  30.5 1.3 %copy-start = (f32[40,80,128]{2,1,0:T(8,128)}, f32[40,80,128]{2,1,0:T(8,128)S(1)}, u32[]{:S(2)}) copy-start(f32[40,80,128]{2,1,0:T(8,128)S(1)} %pad_maximum_fusion.refs_0_) | copy-start | bytes 4915204
  32.2 4.6 %collective-permute-start.5 = (f32[8,40,80]{2,1,0:T(8,128)S(1)}, f32[8,40,80]{2,1,0:T(8,128)S(1)}, u32[]{:S(2)}, u32[]{:S(2)}) collective-permute-start(f32[8,40,80]{2,1,0:T(8,128)S(1)} %copy.6), channel_id=1, source_target_pairs={{0,3},{1,0},{2,1},{3,2},{4,7},{5,4},{6,5},{7,6},{8,11},{9,8},{10,9... | collective-permute-start | bytes 307208 | tf_op jit(solution)/shard_map/ppermute | solution.py:25
  33.6 5.7 %collective-permute-start.6 = (f32[8,40,80]{2,1,0:T(8,128)S(1)}, f32[8,40,80]{2,1,0:T(8,128)}, u32[]{:S(2)}, u32[]{:S(2)}) collective-permute-start(f32[8,40,80]{2,1,0:T(8,128)S(1)} %copy.8), channel_id=1, source_target_pairs={{0,1},{1,2},{2,3},{3,0},{4,5},{5,6},{6,7},{7,4},{8,9},{9,10},{10,1... | collective-permute-start | bytes 307208 | tf_op jit(solution)/shard_map/ppermute | solution.py:25

commit v2 on v1

--- a/solution.py
+++ b/solution.py
@@ -14,88 +14,246 @@
 PAIRS = [(i, j) for i in range(ITERS) for j in range(i, ITERS + 1)]
 
 
-def passed_along(value, axis, steps):
-    count = lax.axis_size(axis)
-    first, last = (max(0, -steps), min(count, count - steps))
-    return lax.ppermute(value, axis, [(source, source + steps) for source in range(first, last)])
-
-
-def around(value, axis, steps):
-    count = lax.axis_size(axis)
-    return lax.ppermute(value, axis, [(i, (i + steps) % count) for i in range(count)])
-
-
-def coupling_terms(couplings):
-    south_rows = passed_along(couplings[:, -1:, :], "gy", 1)
-    extended = jnp.concatenate([south_rows, couplings], axis=1)
-    west_column = around(extended[:, :, -1:], "gx", 1)
-    widened = jnp.concatenate([west_column, extended], axis=2)
-    return (
-        widened[0, 1:, 1:],
-        widened[0, :-1, 1:],
-        widened[1, 1:, 1:],
-        widened[1, 1:, :-1],
-        widened[2, 1:, 1:],
-        widened[2, :-1, 1:],
-        widened[2, 1:, :-1],
-        widened[2, :-1, :-1],
-    )
-
-
-def basis_kernel(members, rows, main_ref, side_ref, diag_ref, basis_ref, gram_ref, sides, gram):
+def slots(lanes, g):
+    return (lanes >= 8 * g) & (lanes < 8 * g + 8)
+
+
+def reversed_tile(x, lanes, subs):
+    for bit in range(7):
+        step = 1 << bit
+        x = jnp.where((lanes & step) == 0, pltpu.roll(x, 128 - step, 1), pltpu.roll(x, step, 1))
+    for bit in range(3):
+        step = 1 << bit
+        x = jnp.where((subs & step) == 0, pltpu.roll(x, 8 - step, 0), pltpu.roll(x, step, 0))
+    return x
+
+
+def halo_kernel(
+    members, ny, nx, rhs, coup, center, mask, main, strips, scale,
+    from_west, from_south, from_corner, rows_s, rows_n, turned, packed, received, send, recv,
+):
+    rows = rhs.shape[1]
+    tiles = rows // 8
+    planes = members + 8
+    y, x = lax.axis_index("gy"), lax.axis_index("gx")
+    north, south = lax.rem(y + 1, ny), lax.rem(y + ny - 1, ny)
+    east, west = lax.rem(x + 1, nx), lax.rem(x + nx - 1, nx)
+    mirror = nx - 1 - x
+    top, bottom = y == ny - 1, y == 0
+    barrier = pltpu.get_barrier_semaphore()
+    peers = ((y, east), (y, west), (north, x), (south, x), (north, east), (south, west), (y, mirror))
+    for there in peers:
+        pl.semaphore_signal(barrier, inc=1, device_id=there, device_id_type=pl.DeviceIdType.MESH)
+    pl.semaphore_wait(barrier, len(peers))
+
+    def copy(src, dst, n, there):
+        return pltpu.make_async_remote_copy(
+            src_ref=src,
+            dst_ref=dst,
+            send_sem=send.at[n],
+            recv_sem=recv.at[n],
+            device_id=there,
+            device_id_type=pl.DeviceIdType.MESH,
+        )
+
+    last_rows = coup.at[:, rows - 8 : rows, :]
+    copies = [
+        copy(coup, from_west, 0, (y, east)),
+        copy(last_rows, from_south, 1, (north, x)),
+        copy(last_rows, from_corner, 2, (north, east)),
+    ]
+    for c in copies:
+        c.start()
+    lanes = lax.broadcasted_iota(jnp.int32, (8, 128), 1)
+    subs = lax.broadcasted_iota(jnp.int32, (8, 128), 0)
+    first = lanes == 0
+    inside = jnp.where(bottom, 0.0, 1.0)
+    for c in copies:
+        c.wait()
+
+    def below(ref, edge, a, t):
+        if t:
+            return ref[a, 8 * t - 1 : 8 * t + 7, :]
+        row = jnp.broadcast_to(edge[a, 7:8, :] * inside, (8, 128))
+        return jnp.where(subs == 0, row, pltpu.roll(ref[a, 0:8, :], 1, 0))
+
+    def westward(here, beside):
+        return jnp.where(first, pltpu.roll(beside, 1, 1), pltpu.roll(here, 1, 1))
+
+    for t in range(tiles):
+        at = slice(8 * t, 8 * t + 8)
+        out = slice(8 * t + HALO, 8 * t + HALO + 8)
+        here = [coup[a, at, :] for a in range(3)]
+        prev = [below(coup, from_south, a, t) for a in range(3)]
+        beside = [from_west[a, at, :] for a in range(3)]
+        corner = below(from_west, from_corner, 2, t)
+        terms = (
+            here[0],
+            prev[0],
+            here[1],
+            westward(here[1], beside[1]),
+            here[2],
+            prev[2],
+            westward(here[2], beside[2]),
+            westward(prev[2], corner),
+        )
+        diag = center[at, :] + sum(terms[1:], terms[0])
+        ocean = mask[at, :].astype(jnp.float32)
+        inverse = ocean / diag
+        scale[at, :] = ocean * diag
+        for d in range(8):
+            main[members + d, out, :] = terms[d] * inverse
+
+        @pl.loop(0, members // 8)
+        def _(block):
+            for within in range(8):
+                m = block * 8 + within
+                main[m, out, :] = rhs[m, at, :] * inverse
+
+    up = copy(main.at[:, rows : rows + 8, :], rows_s, 3, (north, x))
+    down = copy(main.at[:, 8:16, :], rows_n, 4, (south, x))
+    up.start()
+
+    @pl.when(jnp.logical_not(bottom))
+    def _():
+        down.start()
+
+    @pl.when(top)
+    def _():
+        @pl.loop(0, members // 4)
+        def _(block):
+            for within in range(4):
+                m = block * 4 + within
+                turned[m] = reversed_tile(main[m, rows : rows + 8, :], lanes, subs)
+
+        for d in range(8):
+            tile = main[members + OPPOSITE[d], rows : rows + 8, :]
+            turned[members + d] = reversed_tile(tile, lanes, subs)
+        pltpu.make_async_remote_copy(
+            src_ref=turned,
+            dst_ref=rows_n,
+            send_sem=send.at[5],
+            recv_sem=recv.at[4],
+            device_id=(y, mirror),
+            device_id_type=pl.DeviceIdType.MESH,
+        ).start()
+
+    up.wait()
+    down.wait_recv()
+
+    @pl.when(jnp.logical_not(bottom))
+    def _():
+        down.wait_send()
+
+    @pl.when(top)
+    def _():
+        copy(turned, rows_n, 5, (y, mirror)).wait_send()
+
+    main[:, 0:8, :] = rows_s[...] * inside
+    main[:, rows + 8 : rows + 16, :] = rows_n[...]
+
+    @pl.loop(0, tiles + 2)
+    def _(t):
+        at = pl.ds(pl.multiple_of(8 * t, 8), 8)
+        for group in range(3):
+            eastbound = jnp.zeros((8, 128), jnp.float32)
+            westbound = eastbound
+            for g in range(min(16, planes - 16 * group)):
+                v = main[16 * group + g, at, :]
+                slot = slots(lanes, g)
+                eastbound = jnp.where(slot, pltpu.roll(v, (8 * g + 8) % 128, 1), eastbound)
+                westbound = jnp.where(slot, pltpu.roll(v, 8 * g, 1) if g else v, westbound)
+            packed[0, group, at, :] = eastbound
+            packed[1, group, at, :] = westbound
+
+    copies = [
+        copy(packed.at[0], received.at[1], 6, (y, east)),
+        copy(packed.at[1], received.at[0], 7, (y, west)),
+    ]
+    for c in copies:
+        c.start()
+    for c in copies:
+        c.wait()
+    strips[...] = received[...]
+
+
+def basis_kernel(members, rows, main_ref, strip_ref, diag_ref, basis_ref, gram_ref, sides, strip_c, gram):
     tiles = rows // 8
     lanes = lax.broadcasted_iota(jnp.int32, (8, 128), 1)
     first, last = lanes == 0, lanes == 127
+    slot_first, slot_last = lanes % 8 == 0, lanes % 8 == 7
 
     def field(k, m):
         return main_ref.at[m] if k == 0 else basis_ref.at[k - 1, m]
 
-    def side(k, m):
-        return side_ref.at[m] if k == 0 else sides.at[k - 1, m]
+    def side(k, s, group):
+        return strip_ref.at[s, group] if k == 0 else sides.at[k - 1, s, group]
+
+    for tile in range(tiles):
+        at = slice(8 * tile, 8 * tile + 8)
+        for d in range(8):
+            for s in range(2):
+                v = jnp.where(slots(lanes, d), strip_ref[s, 2, at, :], 0.0)
+                for step in (8, 16, 32, 64):
+                    v = v + pltpu.roll(v, step, 1)
+                strip_c[s, d, at, :] = v
+
+    def three(v, before, c, tile):
+        base = 8 * tile
+        mid = v[base : base + 8, :]
+        down = v[base - 1 : base + 7, :] if tile > 0 else pltpu.roll(mid, 1, 0)
+        up = v[base + 1 : base + 9, :] if tile < tiles - 1 else pltpu.roll(mid, 7, 0)
+        centre = c[0] * up + c[1] * down - SHIFT * mid
+        if before is not None:
+            centre = centre - LAG * before[base : base + 8, :]
+        return (
+            centre,
+            c[2] * mid + c[4] * up + c[5] * down,
+            c[3] * mid + c[6] * up + c[7] * down,
+        )
 
     for k in range(ITERS):
-        for tile in range(tiles):
-            base = 8 * tile
-            cm = [main_ref[members + d, base : base + 8, :] for d in range(8)]
-            cs = [side_ref[members + d, base : base + 8, :] for d in range(8)]
-
-            def east(a, b):
-                return jnp.where(last, pltpu.roll(b, 127, 1), pltpu.roll(a, 127, 1))
-
-            def west(a, b):
-                return jnp.where(first, pltpu.roll(b, 1, 1), pltpu.roll(a, 1, 1))
-
+        final = k + 1 == ITERS
+        for tile in range(1, tiles - 1) if final else range(tiles):
+            at = slice(8 * tile, 8 * tile + 8)
+            cm = [main_ref[members + d, at, :] for d in range(8)]
+            ce = [strip_c[0, d, at, :] for d in range(8)]
+            cw = [strip_c[1, d, at, :] for d in range(8)]
             for d in (2, 4, 5):
-                cm[d], cs[d] = west(cm[d], cs[d]), west(cs[d], cm[d])
+                edge = jnp.broadcast_to(cm[d][:, 127:128], (8, 128))
+                ce[d] = jnp.where(slot_first, edge, pltpu.roll(ce[d], 1, 1))
+                cm[d] = jnp.where(first, pltpu.roll(cw[d], 1, 1), pltpu.roll(cm[d], 1, 1))
+                cw[d] = pltpu.roll(cw[d], 1, 1)
             for d in (3, 6, 7):
-                cm[d], cs[d] = east(cm[d], cs[d]), east(cs[d], cm[d])
-
-            @pl.loop(0, members // TOGETHER)
-            def _(block):
-                outs = []
-                for within in range(TOGETHER):
-                    m = block * TOGETHER + within
-                    mids, easts, wests = [], [], []
-                    for get, c in ((field, cm), (side, cs)):
-                        v = get(k, m)
-                        mid = v[base : base + 8, :]
-                        down = v[base - 1 : base + 7, :] if tile > 0 else pltpu.roll(mid, 1, 0)
-                        up = v[base + 1 : base + 9, :] if tile < tiles - 1 else pltpu.roll(mid, 7, 0)
-                        centre = c[0] * up + c[1] * down - SHIFT * mid
-                        if k:
-                            centre = centre - LAG * get(k - 1, m)[base : base + 8, :]
-                        mids.append(centre)
-                        easts.append(c[2] * mid + c[4] * up + c[5] * down)
-                        wests.append(c[3] * mid + c[6] * up + c[7] * down)
-                    rem, res = [pltpu.roll(e, 127, 1) for e in easts]
-                    rwm, rws = [pltpu.roll(w, 1, 1) for w in wests]
-                    out_main = mids[0] + jnp.where(last, res, rem) + jnp.where(first, rws, rwm)
-                    out_side = mids[1] + jnp.where(last, rem, res) + jnp.where(first, rwm, rws)
-                    outs.append((m, out_main, out_side))
-                for m, out_main, out_side in outs:
-                    basis_ref[k, m, base : base + 8, :] = out_main
-                    if k + 1 < ITERS:
-                        sides[k, m, base : base + 8, :] = out_side
+                edge = jnp.broadcast_to(cm[d][:, 0:1], (8, 128))
+                cw[d] = jnp.where(slot_last, edge, pltpu.roll(cw[d], 127, 1))
+                cm[d] = jnp.where(last, pltpu.roll(ce[d], 127, 1), pltpu.roll(cm[d], 127, 1))
+                ce[d] = pltpu.roll(ce[d], 127, 1)
+
+            @pl.loop(0, members // 16)
+            def _(group):
+                before = (lambda s: side(k - 1, s, group)) if k else (lambda s: None)
+                mid_e, e_e, w_e = three(side(k, 0, group), before(0), ce, tile)
+                mid_w, e_w, w_w = three(side(k, 1, group), before(1), cw, tile)
+                into_e, into_w = pltpu.roll(w_e, 1, 1), pltpu.roll(e_w, 127, 1)
+                for block in range(16 // TOGETHER):
+                    outs = []
+                    for g in range(block * TOGETHER, (block + 1) * TOGETHER):
+                        m = group * 16 + g
+                        mid, e, w = three(field(k, m), field(k - 1, m) if k else None, cm, tile)
+                        shift_e = 127 - 8 * g
+                        shift_w = (121 - 8 * g) % 128
+                        out = mid + jnp.where(last, pltpu.roll(e_e, shift_e, 1), pltpu.roll(e, 127, 1))
+                        out = out + jnp.where(first, pltpu.roll(w_w, shift_w, 1), pltpu.roll(w, 1, 1))
+                        outs.append((m, out))
+                        if not final:
+                            into_e = jnp.where(lanes == 8 * g, pltpu.roll(w, 8 * g + 1, 1), into_e)
+                            into_w = jnp.where(lanes == 8 * g + 7, pltpu.roll(e, 8 * g + 7, 1), into_w)
+                    for m, out in outs:
+                        basis_ref[k, m, at, :] = out
+                if not final:
+                    sides[k, 0, group, at, :] = mid_e + pltpu.roll(e_e, 127, 1) + into_e
+                    sides[k, 1, group, at, :] = mid_w + pltpu.roll(w_w, 1, 1) + into_w
 
     @pl.loop(0, members)
     def _(m):
@@ -264,29 +422,38 @@
 
 def on_device(right_side, couplings, center, ocean_mask):
     members, rows, columns = right_side.shape
-    oceanf = ocean_mask.astype(jnp.float32)
-    terms = coupling_terms(couplings)
-    diag = center + sum(terms[1:], terms[0])
-    inverse = oceanf / diag
-    planes = jnp.concatenate([right_side * inverse, jnp.stack(terms) * inverse], axis=0)
-    edge = planes[:, -HALO:, :]
-    south = passed_along(edge, "gy", 1)
-    north = passed_along(planes[:, :HALO, :], "gy", -1)
-    turned = jnp.concatenate([edge[:members]] + [edge[members + d][None] for d in OPPOSITE])
-    turned = turned[:, ::-1, ::-1]
-    count = lax.axis_size("gx")
-    folded = lax.ppermute(turned, "gx", [(i, count - 1 - i) for i in range(count)])
-    top = lax.axis_index("gy") == lax.axis_size("gy") - 1
-    north = jnp.where(top, folded, north)
-    main = jnp.concatenate([south, planes, north], axis=1)
     total = rows + 2 * HALO
-    west = around(jnp.transpose(main[:, :, -HALO:], (2, 0, 1)), "gx", 1)
-    east = around(jnp.transpose(main[:, :, :HALO], (2, 0, 1)), "gx", -1)
-    gap = jnp.zeros((members + 8, total, columns - 2 * HALO), jnp.float32)
-    side = jnp.concatenate(
-        [jnp.transpose(east, (1, 2, 0)), gap, jnp.transpose(west, (1, 2, 0))], axis=2
-    )
+    planes = members + 8
+    ny, nx = lax.axis_size("gy"), lax.axis_size("gx")
     vmem = pl.BlockSpec(memory_space=pltpu.VMEM)
+    f32 = jnp.float32
+
+    def halo(*refs):
+        halo_kernel(members, ny, nx, *refs)
+
+    main, strips, scale = pl.pallas_call(
+        halo,
+        out_shape=(
+            jax.ShapeDtypeStruct((planes, total, columns), f32),
+            jax.ShapeDtypeStruct((2, 3, total, columns), f32),
+            jax.ShapeDtypeStruct((rows, columns), f32),
+        ),
+        in_specs=[vmem] * 4,
+        out_specs=(vmem,) * 3,
+        scratch_shapes=[
+            pltpu.VMEM((3, rows, columns), f32),
+            pltpu.VMEM((3, 8, columns), f32),
+            pltpu.VMEM((3, 8, columns), f32),
+            pltpu.VMEM((planes, 8, columns), f32),
+            pltpu.VMEM((planes, 8, columns), f32),
+            pltpu.VMEM((planes, 8, columns), f32),
+            pltpu.VMEM((2, 3, total, columns), f32),
+            pltpu.VMEM((2, 3, total, columns), f32),
+            pltpu.SemaphoreType.DMA((8,)),
+            pltpu.SemaphoreType.DMA((8,)),
+        ],
+        compiler_params=pltpu.CompilerParams(collective_id=1, has_side_effects=True),
+    )(right_side, couplings, center, ocean_mask)
 
     def first(*refs):
         basis_kernel(members, total, *refs)
@@ -294,16 +461,17 @@
     basis, gram = pl.pallas_call(
         first,
         out_shape=(
-            jax.ShapeDtypeStruct((ITERS, members, total, columns), jnp.float32),
-            jax.ShapeDtypeStruct((8, 128), jnp.float32),
+            jax.ShapeDtypeStruct((ITERS, members, total, columns), f32),
+            jax.ShapeDtypeStruct((8, 128), f32),
         ),
         in_specs=[vmem] * 3,
         out_specs=(vmem, vmem),
         scratch_shapes=[
-            pltpu.VMEM((ITERS - 1, members, total, columns), jnp.float32),
-            pltpu.VMEM((len(PAIRS), members, columns), jnp.float32),
+            pltpu.VMEM((ITERS - 1, 2, 2, total, columns), f32),
+            pltpu.VMEM((2, 8, total, columns), f32),
+            pltpu.VMEM((len(PAIRS), members, columns), f32),
         ],
-    )(main, side, diag)
+    )(main, strips, scale)
     sums = totals(gram)
 
     def second(*refs):
@@ -318,7 +486,7 @@
             pltpu.VMEM((ITERS, members, columns), jnp.float32),
             pltpu.VMEM((ITERS + 1, members, columns), jnp.float32),
         ],
-    )(main, basis, oceanf * diag, sums)
+    )(main, basis, scale, sums)
 
 
 def solution(mesh):

time: 117 us -> 92.7 us (0.79)
  Pallas kernels: 73.6 us -> 91.9 us
  waiting for transfers between devices: 16.7 us -> 0 us
  starting transfers between devices: 12 us -> 0 us
  local copies, waits for them, and re-layouts: 7.41 us -> 0 us
  other arithmetic: 5.3 us -> 0 us
    pallas_call x0 -> x1, Pallas kernels: none -> 27 us  [on_device(): pl.pallas_call(halo, out_shape=(jax.ShapeDtypeStruct((planes, total, colu...]
    ppermute x7 -> x0, waiting for transfers between devices: 16.7 us -> none  [the longest x3 8.43 us: around(): lax.ppermute(value, axis, [(i, (i + steps) % count) for i in range(count)])]
    ppermute x7 -> x0, starting transfers between devices: 12 us -> none  [the longest x3 11 us: passed_along(): lax.ppermute(value, axis, [(source, source + steps) for source in range(f...]
    pallas_call x1, Pallas kernels: 55.1 us -> 47.5 us  [on_device(): pl.pallas_call(first, out_shape=(jax.ShapeDtypeStruct((ITERS, members, to...]
    unnamed x21 -> x0, local copies, waits for them, and re-layouts: 3.07 us -> none
    concatenate x3 -> x0, other arithmetic: 2.75 us -> none  [the longest x1 1.66 us: on_device(): jnp.concatenate([jnp.transpose(east, (1, 2, 0)), gap, jnp.transpose(west,...]
    ppermute x2 -> x0, local copies, waits for them, and re-layouts: 1.92 us -> none  [around(): lax.ppermute(value, axis, [(i, (i + steps) % count) for i in range(count)])]
    mul x3 -> x0, other arithmetic: 1.73 us -> none  [the longest x1 1.63 us: on_device(): oceanf * diag]
  transfers between devices with their start and end apart: 7 -> 0, of which waited for: 7 -> 0; matrix products, arithmetic and copies ran while one was open for 2% -> 0% of each run, Pallas kernels for 0% -> 0%
where the time goes in v2:
time: 92.7 us; the launch traced here: 92.5 us
  Pallas kernels  91.9 us (99%)
    pallas_call x1, Pallas kernels, on_device(): pl.pallas_call(first, out_shape=(jax.ShapeDtypeStruct((ITERS, members, to...  47.5 us
    pallas_call x1, Pallas kernels, on_device(): pl.pallas_call(halo, out_shape=(jax.ShapeDtypeStruct((planes, total, colu...  27 us
    pallas_call x1, Pallas kernels, totals(): pl.pallas_call(kernel, out_shape=jax.ShapeDtypeStruct(values.shape, jnp.f...  10.7 us
    pallas_call x1, Pallas kernels, on_device(): pl.pallas_call(second, out_shape=(jax.ShapeDtypeStruct(right_side.shape,...  6.72 us

profile of v2, /device:TPU:0, one launch (start us, length us, event | category | flops | bytes accessed | tf_op | source)
XLA Modules:
  0.0 92.5 jit_solution(15979736377145400463)
XLA Ops:
  0.6 27.0 %shard_map.59 = (f32[40,80,128]{2,1,0:T(8,128)}, f32[2,3,80,128]{3,2,1,0:T(8,128)}, f32[64,128]{1,0:T(8,128)}) custom-call(f32[32,64,128]{2,1,0:T(8,128)} %refs_0_.1, f32[3,64,128]{2,1,0:T(8,128)} %refs_1_.1, f32[64,128]{1,0:T(8,128)} %refs_2_.1, s32[64,128]{1,0:T(8,128)} %refs_3_.1), custom_call_target="tpu_custom_call" | custom-call | tf_op jit(solution)/shard_map/pallas_call | solution.py:434
  27.6 47.5 %shard_map.60 = (f32[6,32,80,128]{3,2,1,0:T(8,128)}, f32[8,128]{1,0:T(8,128)}) custom-call(f32[40,80,128]{2,1,0:T(8,128)} %get-tuple-element.7.refs_0_, f32[2,3,80,128]{3,2,1,0:T(8,128)} %get-tuple-element.8.refs_1_, f32[64,128]{1,0:T(8,128)} %get-tuple-element.9.refs_2_), custom_call_target="tpu_custom_call" | custom-call | tf_op jit(solution)/shard_map/pallas_call | solution.py:461
  75.1 10.7 %shard_map.61.refs_3_ = f32[8,128]{1,0:T(8,128)} custom-call(f32[8,128]{1,0:T(8,128)} %get-tuple-element.11.refs_0_), custom_call_target="tpu_custom_call" | custom-call | tf_op jit(solution)/shard_map/pallas_call | solution.py:411
  85.8 6.7 %shard_map.62 = (f32[32,64,128]{2,1,0:T(8,128)}, f32[32,64,128]{2,1,0:T(8,128)}) custom-call(f32[40,80,128]{2,1,0:T(8,128)} %get-tuple-element.7.refs_0_, f32[6,32,80,128]{3,2,1,0:T(8,128)} %get-tuple-element.10.refs_1_, f32[64,128]{1,0:T(8,128)} %get-tuple-element.9.refs_2_, f32[8,128]{1,0:T(8,128)} %shard_map.61.refs_3_), custom_call_target="tpu_custom_call" | custom-call | tf_op jit(solution)/shard_map/pallas_call | solution.py:480

commit v3 on v2

--- a/solution.py
+++ b/solution.py
@@ -9,7 +9,8 @@
 HALO = 8
 SHIFT = 0.1
 LAG = 0.05
-TOGETHER = 4
+TOGETHER = 8
+GRANT = 20 * 1024 * 1024
 OPPOSITE = (1, 0, 3, 2, 7, 6, 5, 4)
 PAIRS = [(i, j) for i in range(ITERS) for j in range(i, ITERS + 1)]
 
@@ -177,17 +178,19 @@
     strips[...] = received[...]
 
 
-def basis_kernel(members, rows, main_ref, strip_ref, diag_ref, basis_ref, gram_ref, sides, strip_c, gram):
+def basis_kernel(members, rows, main_ref, strip_ref, diag_ref, *refs):
+    basis, gram_ref = refs[:ITERS], refs[ITERS]
+    sides, (strip_c, gram) = refs[ITERS + 1 : 2 * ITERS], refs[2 * ITERS :]
     tiles = rows // 8
     lanes = lax.broadcasted_iota(jnp.int32, (8, 128), 1)
     first, last = lanes == 0, lanes == 127
     slot_first, slot_last = lanes % 8 == 0, lanes % 8 == 7
 
     def field(k, m):
-        return main_ref.at[m] if k == 0 else basis_ref.at[k - 1, m]
+        return main_ref.at[m] if k == 0 else basis[k - 1].at[m]
 
     def side(k, s, group):
-        return strip_ref.at[s, group] if k == 0 else sides.at[k - 1, s, group]
+        return strip_ref.at[s, group] if k == 0 else sides[k - 1].at[s, group]
 
     for tile in range(tiles):
         at = slice(8 * tile, 8 * tile + 8)
@@ -250,10 +253,10 @@
                             into_e = jnp.where(lanes == 8 * g, pltpu.roll(w, 8 * g + 1, 1), into_e)
                             into_w = jnp.where(lanes == 8 * g + 7, pltpu.roll(e, 8 * g + 7, 1), into_w)
                     for m, out in outs:
-                        basis_ref[k, m, at, :] = out
+                        basis[k][m, at, :] = out
                 if not final:
-                    sides[k, 0, group, at, :] = mid_e + pltpu.roll(e_e, 127, 1) + into_e
-                    sides[k, 1, group, at, :] = mid_w + pltpu.roll(w_w, 1, 1) + into_w
+                    sides[k][0, group, at, :] = mid_e + pltpu.roll(e_e, 127, 1) + into_e
+                    sides[k][1, group, at, :] = mid_w + pltpu.roll(w_w, 1, 1) + into_w
 
     @pl.loop(0, members)
     def _(m):
@@ -377,7 +380,8 @@
     return x, z
 
 
-def combine_kernel(members, rows, z_ref, basis_ref, scale_ref, sum_ref, x_ref, r_ref, cx, cz):
+def combine_kernel(members, rows, z_ref, *refs):
+    basis, (scale_ref, sum_ref, x_ref, r_ref, cx, cz) = refs[:ITERS], refs[ITERS:]
     gram = [[None] * (ITERS + 1) for _ in range(ITERS + 1)]
     sums = unpacked(sum_ref[...], members)
     for n, (i, j) in enumerate(PAIRS):
@@ -394,7 +398,7 @@
         zs = [jnp.broadcast_to(cz[k, pl.ds(m, 1), :], (8, 128)) for k in range(ITERS + 1)]
         for base in range(0, rows, 8):
             at = slice(base + HALO, base + HALO + 8)
-            vs = [z_ref[m, at, :]] + [basis_ref[k, m, at, :] for k in range(ITERS)]
+            vs = [z_ref[m, at, :]] + [basis[k][m, at, :] for k in range(ITERS)]
             x_ref[m, base : base + 8, :] = sum((xs[k] * vs[k] for k in range(1, ITERS)), xs[0] * vs[0])
             total = sum((zs[k] * vs[k] for k in range(1, ITERS + 1)), zs[0] * vs[0])
             r_ref[m, base : base + 8, :] = scale_ref[base : base + 8, :] * total
@@ -416,7 +420,9 @@
         scratch_shapes=[pltpu.VMEM((count,) + values.shape, jnp.float32) for count in counts]
         + [pltpu.VMEM(values.shape, jnp.float32)]
         + [pltpu.SemaphoreType.DMA((count,)) for count in counts] * 2,
-        compiler_params=pltpu.CompilerParams(collective_id=0, has_side_effects=True),
+        compiler_params=pltpu.CompilerParams(
+            collective_id=0, has_side_effects=True, vmem_limit_bytes=GRANT
+        ),
     )(values)
 
 
@@ -452,22 +458,23 @@
             pltpu.SemaphoreType.DMA((8,)),
             pltpu.SemaphoreType.DMA((8,)),
         ],
-        compiler_params=pltpu.CompilerParams(collective_id=1, has_side_effects=True),
+        compiler_params=pltpu.CompilerParams(
+            collective_id=1, has_side_effects=True, vmem_limit_bytes=GRANT
+        ),
     )(right_side, couplings, center, ocean_mask)
 
     def first(*refs):
         basis_kernel(members, total, *refs)
 
-    basis, gram = pl.pallas_call(
+    *basis, gram = pl.pallas_call(
         first,
-        out_shape=(
-            jax.ShapeDtypeStruct((ITERS, members, total, columns), f32),
-            jax.ShapeDtypeStruct((8, 128), f32),
-        ),
+        out_shape=(jax.ShapeDtypeStruct((members, total, columns), f32),) * ITERS
+        + (jax.ShapeDtypeStruct((8, 128), f32),),
         in_specs=[vmem] * 3,
-        out_specs=(vmem, vmem),
-        scratch_shapes=[
-            pltpu.VMEM((ITERS - 1, 2, 2, total, columns), f32),
+        out_specs=(vmem,) * (ITERS + 1),
+        compiler_params=pltpu.CompilerParams(vmem_limit_bytes=GRANT),
+        scratch_shapes=[pltpu.VMEM((2, 2, total, columns), f32)] * (ITERS - 1)
+        + [
             pltpu.VMEM((2, 8, total, columns), f32),
             pltpu.VMEM((len(PAIRS), members, columns), f32),
         ],
@@ -480,13 +487,14 @@
     return pl.pallas_call(
         second,
         out_shape=(jax.ShapeDtypeStruct(right_side.shape, jnp.float32),) * 2,
-        in_specs=[vmem] * 4,
+        in_specs=[vmem] * (ITERS + 3),
         out_specs=(vmem, vmem),
+        compiler_params=pltpu.CompilerParams(vmem_limit_bytes=GRANT),
         scratch_shapes=[
             pltpu.VMEM((ITERS, members, columns), jnp.float32),
             pltpu.VMEM((ITERS + 1, members, columns), jnp.float32),
         ],
-    )(main, basis, scale, sums)
+    )(main, *basis, scale, sums)
 
 
 def solution(mesh):

time: 92.7 us -> 84.6 us (0.913)
  Pallas kernels: 91.9 us -> 80 us
  local copies, waits for them, and re-layouts: 0 us -> 3.62 us
    pallas_call x1, Pallas kernels: 47.5 us -> 43 us  [on_device(): pl.pallas_call(first, out_shape=(jax.ShapeDtypeStruct((members, total, co...]
    pallas_call x1, Pallas kernels: 6.72 us -> 3.04 us  [on_device(): pl.pallas_call(second, out_shape=(jax.ShapeDtypeStruct(right_side.shape,...]
    unnamed x0 -> x8, local copies, waits for them, and re-layouts: none -> 3.62 us
    pallas_call x1, Pallas kernels: 27 us -> 24.4 us  [on_device(): pl.pallas_call(halo, out_shape=(jax.ShapeDtypeStruct((planes, total, colu...]
    pallas_call x1, Pallas kernels: 10.7 us -> 9.52 us  [totals(): pl.pallas_call(kernel, out_shape=jax.ShapeDtypeStruct(values.shape, jnp.f...]
where the time goes in v3:
time: 84.6 us; the launch traced here: 84.3 us
  Pallas kernels  80 us (95%)
  local copies, waits for them, and re-layouts  3.62 us (4%)
    pallas_call x1, Pallas kernels, on_device(): pl.pallas_call(first, out_shape=(jax.ShapeDtypeStruct((members, total, co...  43 us
    pallas_call x1, Pallas kernels, on_device(): pl.pallas_call(halo, out_shape=(jax.ShapeDtypeStruct((planes, total, colu...  24.4 us
    pallas_call x1, Pallas kernels, totals(): pl.pallas_call(kernel, out_shape=jax.ShapeDtypeStruct(values.shape, jnp.f...  9.52 us
    unnamed x8, local copies, waits for them, and re-layouts  3.62 us
    pallas_call x1, Pallas kernels, on_device(): pl.pallas_call(second, out_shape=(jax.ShapeDtypeStruct(right_side.shape,...  3.04 us

profile of v3, /device:TPU:0, one launch (start us, length us, event | category | flops | bytes accessed | tf_op | source)
XLA Modules:
  0.0 84.3 jit_solution(10912695399732398483)
XLA Ops:
  0.6 0.0 copy-start
  0.6 1.2 %copy-done = f32[32,64,128]{2,1,0:T(8,128)S(1)} copy-done((f32[32,64,128]{2,1,0:T(8,128)S(1)}, f32[32,64,128]{2,1,0:T(8,128)}, u32[]{:S(2)}) %copy-start) | copy-done | bytes 1048600
  1.9 0.0 copy-start.1
  1.9 0.9 %copy-done.1 = f32[3,64,128]{2,1,0:T(8,128)S(1)} copy-done((f32[3,64,128]{2,1,0:T(8,128)S(1)}, f32[3,64,128]{2,1,0:T(8,128)}, u32[]{:S(2)}) %copy-start.1) | copy-done | bytes 98328
  2.7 0.0 copy-start.2
  2.8 0.8 copy-done.2
  3.5 0.0 copy-start.3
  3.5 0.8 copy-done.3
  4.3 24.4 %shard_map.59 = (f32[40,80,128]{2,1,0:T(8,128)S(1)}, f32[2,3,80,128]{3,2,1,0:T(8,128)S(1)}, f32[64,128]{1,0:T(8,128)S(1)}) custom-call(f32[32,64,128]{2,1,0:T(8,128)S(1)} %copy-done, f32[3,64,128]{2,1,0:T(8,128)S(1)} %copy-done.1, f32[64,128]{1,0:T(8,128)S(1)} %copy-done.2, s32[64,128]{1,0:T(8,128)S(1)} %copy-done.3), custom_call_target="tpu_custom_call" | custom-call | tf_op jit(solution)/shard_map/pallas_call | solution.py:440
  28.7 43.0 %shard_map.60 = (f32[32,80,128]{2,1,0:T(8,128)S(1)}, f32[32,80,128]{2,1,0:T(8,128)S(1)}, f32[32,80,128]{2,1,0:T(8,128)S(1)}, f32[32,80,128]{2,1,0:T(8,128)S(1)},...) custom-call(f32[40,80,128]{2,1,0:T(8,128)S(1)} %get-tuple-element.12.refs_0_, ...), custom_call_target="tpu_custom_call" | custom-call | tf_op jit(solution)/shard_map/pallas_call | solution.py:469
  71.7 9.5 %shard_map.61.refs_8_ = f32[8,128]{1,0:T(8,128)S(1)} custom-call(f32[8,128]{1,0:T(8,128)S(1)} %get-tuple-element.21.refs_0_), custom_call_target="tpu_custom_call" | custom-call | tf_op jit(solution)/shard_map/pallas_call | solution.py:415
  81.2 3.0 %shard_map.62 = (f32[32,64,128]{2,1,0:T(8,128)}, f32[32,64,128]{2,1,0:T(8,128)}) custom-call(f32[40,80,128]{2,1,0:T(8,128)S(1)} %get-tuple-element.12.refs_0_, f32[32,80,128]{2,1,0:T(8,128)S(1)} %get-tuple-element.15.refs_1_, f32[32,80,128]{2,1,0:T(8,128)S(1)} %get-tuple-element.16.refs_2_, f32[32,80,128]{2,1,0:T(8,128)S(1)} %get-tuple-element.17.refs_3_, ...), custom_call_target="tpu_custom_call" | custom-call | tf_op jit(solution)/shard_map/pallas_call | solution.py:487
Async XLA Ops:
  0.6 1.2 %copy-start = (f32[32,64,128]{2,1,0:T(8,128)S(1)}, f32[32,64,128]{2,1,0:T(8,128)}, u32[]{:S(2)}) copy-start(f32[32,64,128]{2,1,0:T(8,128)} %refs_0_.1) | copy-start | bytes 3145732
  1.9 0.9 %copy-start.1 = (f32[3,64,128]{2,1,0:T(8,128)S(1)}, f32[3,64,128]{2,1,0:T(8,128)}, u32[]{:S(2)}) copy-start(f32[3,64,128]{2,1,0:T(8,128)} %refs_1_.1) | copy-start | bytes 294916
  2.7 0.8 copy-start.2
  3.5 0.8 copy-start.3

commit v4 on v3

--- a/solution.py
+++ b/solution.py
@@ -30,11 +30,15 @@
 
 
 def halo_kernel(
-    members, ny, nx, rhs, coup, center, mask, main, strips, scale,
-    from_west, from_south, from_corner, rows_s, rows_n, turned, packed, received, send, recv,
+    members, ny, nx, rhs_in, coup_in, center_in, mask_in, main, strips, scale,
+    rhs, coup, center, mask, load, from_west, from_south, from_corner, rows_s, rows_n, turned, packed, received, send, recv,
 ):
     rows = rhs.shape[1]
     tiles = rows // 8
+    pairs = ((coup_in, coup), (center_in, center), (mask_in, mask), (rhs_in, rhs))
+    loads = [pltpu.make_async_copy(a, b, load.at[n]) for n, (a, b) in enumerate(pairs)]
+    for c in loads:
+        c.start()
     planes = members + 8
     y, x = lax.axis_index("gy"), lax.axis_index("gx")
     north, south = lax.rem(y + 1, ny), lax.rem(y + ny - 1, ny)
@@ -57,6 +61,7 @@
             device_id_type=pl.DeviceIdType.MESH,
         )
 
+    loads[0].wait()
     last_rows = coup.at[:, rows - 8 : rows, :]
     copies = [
         copy(coup, from_west, 0, (y, east)),
@@ -69,7 +74,7 @@
     subs = lax.broadcasted_iota(jnp.int32, (8, 128), 0)
     first = lanes == 0
     inside = jnp.where(bottom, 0.0, 1.0)
-    for c in copies:
+    for c in loads[1:] + copies:
         c.wait()
 
     def below(ref, edge, a, t):
@@ -444,9 +449,14 @@
             jax.ShapeDtypeStruct((2, 3, total, columns), f32),
             jax.ShapeDtypeStruct((rows, columns), f32),
         ),
-        in_specs=[vmem] * 4,
+        in_specs=[pl.BlockSpec(memory_space=pltpu.HBM)] * 4,
         out_specs=(vmem,) * 3,
         scratch_shapes=[
+            pltpu.VMEM(right_side.shape, f32),
+            pltpu.VMEM(couplings.shape, f32),
+            pltpu.VMEM(center.shape, f32),
+            pltpu.VMEM(ocean_mask.shape, ocean_mask.dtype),
+            pltpu.SemaphoreType.DMA((4,)),
             pltpu.VMEM((3, rows, columns), f32),
             pltpu.VMEM((3, 8, columns), f32),
             pltpu.VMEM((3, 8, columns), f32),

time: 84.6 us -> 84.9 us (level)
  no operation moved by 1% of the time
where the time goes in v4:
time: 84.9 us; the launch traced here: 84.5 us
  Pallas kernels  80.3 us (95%)
  local copies, waits for them, and re-layouts  3.62 us (4%)
    pallas_call x1, Pallas kernels, on_device(): pl.pallas_call(first, out_shape=(jax.ShapeDtypeStruct((members, total, co...  43 us
    pallas_call x1, Pallas kernels, on_device(): pl.pallas_call(halo, out_shape=(jax.ShapeDtypeStruct((planes, total, colu...  24.6 us
    pallas_call x1, Pallas kernels, totals(): pl.pallas_call(kernel, out_shape=jax.ShapeDtypeStruct(values.shape, jnp.f...  9.55 us
    unnamed x8, local copies, waits for them, and re-layouts  3.62 us
    pallas_call x1, Pallas kernels, on_device(): pl.pallas_call(second, out_shape=(jax.ShapeDtypeStruct(right_side.shape,...  3.04 us

profile of v4, /device:TPU:0, one launch (start us, length us, event | category | flops | bytes accessed | tf_op | source)
XLA Modules:
  0.0 84.5 jit_solution(4808952051381125173)
XLA Ops:
  0.6 0.0 copy-start
  0.6 1.2 %copy-done = f32[32,64,128]{2,1,0:T(8,128)S(1)} copy-done((f32[32,64,128]{2,1,0:T(8,128)S(1)}, f32[32,64,128]{2,1,0:T(8,128)}, u32[]{:S(2)}) %copy-start) | copy-done | bytes 1048600
  1.9 0.0 copy-start.1
  1.9 0.9 %copy-done.1 = f32[3,64,128]{2,1,0:T(8,128)S(1)} copy-done((f32[3,64,128]{2,1,0:T(8,128)S(1)}, f32[3,64,128]{2,1,0:T(8,128)}, u32[]{:S(2)}) %copy-start.1) | copy-done | bytes 98328
  2.7 0.0 copy-start.2
  2.8 0.8 copy-done.2
  3.5 0.0 copy-start.3
  3.5 0.8 copy-done.3
  4.3 24.6 %shard_map.59 = (f32[40,80,128]{2,1,0:T(8,128)S(1)}, f32[2,3,80,128]{3,2,1,0:T(8,128)S(1)}, f32[64,128]{1,0:T(8,128)S(1)}) custom-call(f32[32,64,128]{2,1,0:T(8,128)S(1)} %copy-done, f32[3,64,128]{2,1,0:T(8,128)S(1)} %copy-done.1, f32[64,128]{1,0:T(8,128)S(1)} %copy-done.2, s32[64,128]{1,0:T(8,128)S(1)} %copy-done.3), custom_call_target="tpu_custom_call" | custom-call | tf_op jit(solution)/shard_map/pallas_call | solution.py:445
  28.9 43.0 %shard_map.60 = (f32[32,80,128]{2,1,0:T(8,128)S(1)}, f32[32,80,128]{2,1,0:T(8,128)S(1)}, f32[32,80,128]{2,1,0:T(8,128)S(1)}, f32[32,80,128]{2,1,0:T(8,128)S(1)},...) custom-call(f32[40,80,128]{2,1,0:T(8,128)S(1)} %get-tuple-element.12.refs_0_, ...), custom_call_target="tpu_custom_call" | custom-call | tf_op jit(solution)/shard_map/pallas_call | solution.py:479
  71.9 9.5 %shard_map.61.refs_8_ = f32[8,128]{1,0:T(8,128)S(1)} custom-call(f32[8,128]{1,0:T(8,128)S(1)} %get-tuple-element.21.refs_0_), custom_call_target="tpu_custom_call" | custom-call | tf_op jit(solution)/shard_map/pallas_call | solution.py:420
  81.5 3.0 %shard_map.62 = (f32[32,64,128]{2,1,0:T(8,128)}, f32[32,64,128]{2,1,0:T(8,128)}) custom-call(f32[40,80,128]{2,1,0:T(8,128)S(1)} %get-tuple-element.12.refs_0_, f32[32,80,128]{2,1,0:T(8,128)S(1)} %get-tuple-element.15.refs_1_, f32[32,80,128]{2,1,0:T(8,128)S(1)} %get-tuple-element.16.refs_2_, f32[32,80,128]{2,1,0:T(8,128)S(1)} %get-tuple-element.17.refs_3_, ...), custom_call_target="tpu_custom_call" | custom-call | tf_op jit(solution)/shard_map/pallas_call | solution.py:497
Async XLA Ops:
  0.6 1.2 %copy-start = (f32[32,64,128]{2,1,0:T(8,128)S(1)}, f32[32,64,128]{2,1,0:T(8,128)}, u32[]{:S(2)}) copy-start(f32[32,64,128]{2,1,0:T(8,128)} %refs_0_.1) | copy-start | bytes 3145732
  1.9 0.9 %copy-start.1 = (f32[3,64,128]{2,1,0:T(8,128)S(1)}, f32[3,64,128]{2,1,0:T(8,128)}, u32[]{:S(2)}) copy-start(f32[3,64,128]{2,1,0:T(8,128)} %refs_1_.1) | copy-start | bytes 294916
  2.7 0.8 copy-start.2
  3.5 0.8 copy-start.3
